TPU v7x, 256 devices: a whole 4x4x8 slice. The times are simulated.
256 devices in a mesh: grp: 32 (over z, y_hi, core), seq: 8 (over y_lo, x).
Axes of the slice: x: 4, y: 4 (y_hi: 2, y_lo: 2; y = y_hi * 2 + y_lo), z: 8, core: 2. Of those that a mesh axis runs over, the one named last changes fastest.
Arguments:
- queries: bfloat16 [65536, 4096], P(('grp', 'seq')), may hold values from -8 to 8
- keys: bfloat16 [65536, 4096], P(('grp', 'seq')), may hold values from -6 to 6
- values: bfloat16 [65536, 4096], P(('grp', 'seq')), may hold values from -6 to 6
- global_pos: int32 [512], P(('grp', 'seq')), may hold values from 0 to 127
- layout: int32 [512, 32], P(('grp', 'seq')), may hold values from 0 to 511, all different within a row
Outputs:
- attended: bfloat16 [65536, 4096], P(('grp', 'seq'))
Inputs may be any that keep to these rules, and one draw needn't show every extreme that they name: `layout`: each row lists 32 different block indices, and every block is listed by some row.
All inputs are finite; a program needn't handle non-finite values.
Results may differ from a plain program's by a relative error of at most 0.0042.
Values may be sent and summed in bfloat16 or wider, within the bound.
A program may use at most 128 MiB of HBM per device.

v0:
```python
import math

import jax
import jax.numpy as jnp
from jax import lax
from jax.sharding import PartitionSpec as P

HEADS = 32
HEAD_DIM = 128
BLOCK = 128


def shifted(value, axis, by):
    count = lax.axis_size(axis)
    pairs = [(i, i + by) for i in range(count) if 0 <= i + by < count]
    return lax.ppermute(value, axis, pairs)


def copy_for_each(value, axis):
    copies = jnp.broadcast_to(value, (lax.axis_size(axis), *value.shape))
    return lax.all_to_all(copies, axis, split_axis=0, concat_axis=0, tiled=True)


def laid_out(blocks, dim):
    lengths = list(blocks.shape[1:])
    lengths[dim] *= blocks.shape[0]
    return jnp.moveaxis(blocks, 0, dim).reshape(lengths)


def gather_directly(value, axis, dim):
    blocks = copy_for_each(value, axis)
    return laid_out(blocks, dim)


def sent_together(arrays, axis, dim, along):
    both = jnp.concatenate(arrays, axis=along)
    result, at, gathered = (gather_directly(both, axis, dim), 0, [])
    for a in arrays:
        gathered.append(lax.slice_in_dim(result, at, at + a.shape[along], axis=along))
        at += a.shape[along]
    return tuple(gathered)


def side_by_side(arrays, axis, dim, along):
    widths = [a.shape[along] for a in arrays]
    both = jnp.concatenate(arrays, axis=along)
    result = lax.all_gather(both, axis, axis=dim, tiled=True)
    return tuple(jnp.split(result, [sum(widths[:k]) for k in range(1, len(widths))], axis=along))


def pooled(source, blocks_dev):
    blocks = source.astype(jnp.float32).reshape(blocks_dev, BLOCK, HEADS, HEAD_DIM).mean(axis=1)
    spread = jnp.mean(blocks * blocks, axis=-1, keepdims=True)
    return (
        (blocks / jnp.sqrt(spread + 1e-06))
        .reshape(blocks_dev, HEADS * HEAD_DIM)
        .astype(jnp.bfloat16)
    )


def shards(queries, keys, values, global_pos, layout):
    rows_dev, model_width = queries.shape
    blocks_dev = rows_dev // BLOCK
    devices = lax.axis_size(("grp", "seq"))
    position = lax.axis_index(("grp", "seq"))
    score_scale = 1.0 / math.sqrt(HEAD_DIM)
    summary_keys = pooled(keys, blocks_dev)
    summary_values = pooled(values, blocks_dev)
    edge_last = jnp.stack([keys[rows_dev - BLOCK :], values[rows_dev - BLOCK :]])
    edge_first = jnp.stack([keys[:BLOCK], values[:BLOCK]])
    from_left = shifted(edge_last, ("grp", "seq"), 1)
    from_right = shifted(edge_first, ("grp", "seq"), -1)
    wide_keys = jnp.concatenate([from_left[0], keys, from_right[0]], axis=0)
    wide_values = jnp.concatenate([from_left[1], values, from_right[1]], axis=0)
    window_keys = jnp.stack(
        [wide_keys[block_at * BLOCK : (block_at + 3) * BLOCK] for block_at in range(blocks_dev)]
    )
    window_values = jnp.stack(
        [wide_values[block_at * BLOCK : (block_at + 3) * BLOCK] for block_at in range(blocks_dev)]
    )
    window_keys = window_keys.reshape(blocks_dev, 3 * BLOCK, HEADS, HEAD_DIM)
    window_values = window_values.reshape(blocks_dev, 3 * BLOCK, HEADS, HEAD_DIM)
    query_blocks = queries.reshape(blocks_dev, BLOCK, HEADS, HEAD_DIM)
    scores = (
        jnp.einsum("bqhd,bkhd->bhqk", query_blocks, window_keys, preferred_element_type=jnp.float32)
        * score_scale
    )
    key_block = (
        position * blocks_dev
        + jnp.arange(blocks_dev, dtype=jnp.int32)[:, None]
        + jnp.arange(3 * BLOCK, dtype=jnp.int32)[None, :] // BLOCK
        - 1
    )
    inside = (key_block >= 0) & (key_block < devices * blocks_dev)
    scores = jnp.where(inside[:, None, None, :], scores, -jnp.inf)
    peak = jnp.max(scores, axis=-1)
    weights = jnp.exp(scores - peak[..., None])
    totals = jnp.sum(weights, axis=-1)
    numerator = jnp.einsum(
        "bhqk,bkhd->bhqd",
        weights.astype(jnp.bfloat16),
        window_values,
        preferred_element_type=jnp.float32,
    )
    is_global = jnp.arange(BLOCK, dtype=jnp.int32)[None, :] == global_pos[:, None]
    group_keys, group_values = sent_together((summary_keys, summary_values), "seq", 0, 1)
    piece_keys, piece_values = side_by_side((group_keys, group_values), "grp", 0, 1)
    length = piece_keys.shape[0]
    block_ids = jnp.arange(length, dtype=jnp.int32)
    listed = jnp.any(layout[:, :, None] == block_ids[None, None, :], axis=1)
    visible = listed[:, None, :] | is_global[:, :, None]
    part_scores = (
        jnp.einsum(
            "bqhd,jhd->bhqj",
            query_blocks,
            piece_keys.reshape(length, HEADS, HEAD_DIM),
            preferred_element_type=jnp.float32,
        )
        * score_scale
    )
    part_scores = jnp.where(visible[:, None, :, :], part_scores, -jnp.inf)
    new_peak = jnp.maximum(peak, jnp.max(part_scores, axis=-1))
    factor = jnp.exp(peak - new_peak)
    part_weights = jnp.exp(part_scores - new_peak[..., None])
    totals_next = totals * factor + jnp.sum(part_weights, axis=-1)
    numerator_next = numerator * factor[..., None] + jnp.einsum(
        "bhqj,jhd->bhqd",
        part_weights.astype(jnp.bfloat16),
        piece_values.reshape(length, HEADS, HEAD_DIM),
        preferred_element_type=jnp.float32,
    )
    result = numerator_next / totals_next[..., None]
    return jnp.transpose(result, (0, 2, 1, 3)).reshape(rows_dev, model_width).astype(jnp.bfloat16)


def solution(mesh):
    in_specs = (
        P(("grp", "seq"), None),
        P(("grp", "seq"), None),
        P(("grp", "seq"), None),
        P(("grp", "seq")),
        P(("grp", "seq"), None),
    )
    out_specs = P(("grp", "seq"), None)
    return jax.shard_map(shards, mesh=mesh, in_specs=in_specs, out_specs=out_specs, check_vma=False)
```

profile of v0, /device:TPU:1, one launch (start us, length us, event | category | flops | bytes accessed | tf_op | source)
XLA Modules:
  0.0 242.0 jit_solution(13085365562226667311)
XLA Ops:
  6.5 2.1 convert_bitcast_fusion
  12.9 11.9 %all_to_all.5 = bf16[8,2,8192]{2,1,0:T(2,128)(2,1)S(1)} all-to-all(bf16[8,2,8192]{2,1,0:T(2,128)(2,1)S(1)} %broadcast_in_dim.25), channel_id=1, replica_groups=mesh['grp'=32,'seq'=8] {'seq'}, dimensions={0} | all-to-all | bytes 524288 | tf_op jit(solution)/shard_map/all_to_all | solution.py:21
  25.7 3.3 %copy.90 = bf16[256,4096]{0,1:T(8,128)(2,1)S(1)} copy(bf16[256,4096]{1,0:T(8,128)(2,1)} %param.7) | data formatting | bytes 4194304 | tf_op args[2]
  29.0 4.1 %copy.89 = bf16[256,4096]{0,1:T(8,128)(2,1)} copy(bf16[256,4096]{1,0:T(8,128)(2,1)} %param.6) | data formatting | bytes 4194304 | tf_op args[1]
  33.0 2.0 slice_bitcast_fusion.2
  35.1 1.5 pad_maximum_fusion.1
  36.6 4.9 %collective-permute-start.1 = (bf16[2,128,4096]{1,2,0:T(8,128)(2,1)}, bf16[2,128,4096]{1,2,0:T(8,128)(2,1)}, u32[]{:S(2)}, u32[]{:S(2)}) collective-permute-start(bf16[2,128,4096]{1,2,0:T(8,128)(2,1)} %pad_maximum_fusion.1), channel_id=1, source_target_pairs={{1,0},{2,1},{3,2},{4,3},{5,4},{6,5},{7,6},{8,7},{9,8},{10,9},{11,1... | collective-permute-start | bytes 6291464 | tf_op jit(solution)/shard_map/ppermute | solution.py:16
  41.5 1.5 pad_maximum_fusion
  43.0 2.1 collective-permute-start
  45.1 1.8 copy.123
  47.0 4.1 %copy.93 = bf16[1,256,32,128]{3,1,2,0:T(8,128)(2,1)} copy(bf16[1,256,32,128]{1,3,2,0:T(8,128)(2,1)} %bitcast.95) | data formatting | bytes 4194304 | tf_op jit(solution)/shard_map/concatenate | solution.py:73
  51.0 2.9 %copy.101 = bf16[1,256,32,128]{3,1,2,0:T(8,128)(2,1)} copy(bf16[1,256,32,128]{1,3,2,0:T(8,128)(2,1)S(1)} %bitcast.94) | data formatting | bytes 4194304 | tf_op jit(solution)/shard_map/concatenate | solution.py:74
  54.4 32.8 %collective-permute-done.1 = bf16[2,128,4096]{1,2,0:T(8,128)(2,1)} collective-permute-done((bf16[2,128,4096]{1,2,0:T(8,128)(2,1)}, bf16[2,128,4096]{1,2,0:T(8,128)(2,1)}, u32[]{:S(2)}, u32[]{:S(2)}) %collective-permute-start.1) | collective-permute-done | bytes 2097184 | tf_op jit(solution)/shard_map/ppermute | solution.py:16
  87.2 1.7 fusion.52
  88.9 1.3 copy.97
  90.2 4.1 %collective-permute-done = bf16[2,128,4096]{1,2,0:T(8,128)(2,1)} collective-permute-done((bf16[2,128,4096]{1,2,0:T(8,128)(2,1)}, bf16[2,128,4096]{1,2,0:T(8,128)(2,1)}, u32[]{:S(2)}, u32[]{:S(2)}) %collective-permute-start) | collective-permute-done | bytes 2097184 | tf_op jit(solution)/shard_map/ppermute | solution.py:16
  94.4 3.0 %fusion.51 = (bf16[1,128,4096]{1,2,0:T(8,128)(2,1)}, bf16[1,128,4096]{1,2,0:T(8,128)(2,1)}) fusion(bf16[2,128,4096]{1,2,0:T(8,128)(2,1)} %collective-permute-done), kind=kLoop, calls=%fused_computation.85 | loop fusion | bytes 4194304 | tf_op jit(solution)/shard_map/slice | solution.py:74
  97.4 2.4 %copy.92 = bf16[1,128,32,128]{3,1,2,0:T(8,128)(2,1)} copy(bf16[1,128,32,128]{1,3,2,0:T(8,128)(2,1)} %bitcast.106) | data formatting | bytes 2097152 | tf_op jit(solution)/shard_map/concatenate | solution.py:73
  101.1 2.3 copy.100
  103.4 6.2 %bitcast_reduce_fusion = (f32[2,32,128]{2,1,0:T(8,128)S(1)}, f32[2,32,384,128]{3,2,1,0:T(8,128)S(1)}) fusion(pred[2,384]{1,0:T(4,128)(4,1)S(1)} %compare_and_fusion, bf16[2,128,32,128]{3,2,1,0:T(8,128)(2,1)S(1)} %bitcast.101, bf16[1,128,32,128]{3,1,2,0:T(8,128)(2,1)} %copy.97, bf16[1,256,32,128]{3,1,2,0:T(8,128)(2,1)} %copy.93, ...), kind=kOutput, calls=%fused_computation.6 | convolution fusion | flops 839901184 | bytes 18907904 | tf_op jit(solution)/shard_map/bqhd,bkhd->bhqk/dot_general | solution.py:85
  109.6 4.6 %copy-done = f32[2,32,384,128]{3,2,1,0:T(8,128)} copy-done((f32[2,32,384,128]{3,2,1,0:T(8,128)}, f32[2,32,384,128]{3,2,1,0:T(8,128)S(1)}, u32[]{:S(2)}) %copy-start) | copy-done | bytes 12582936
  114.2 3.8 %fusion.4 = f32[2,32,128]{2,1,0:T(8,128)S(1)} fusion(f32[2,32,384,128]{3,2,1,0:T(8,128)S(1)} %get-tuple-element.20, f32[2,32,128]{2,1,0:T(8,128)S(1)} %get-tuple-element.19, pred[2,384]{1,0:T(4,128)(4,1)S(1)} %compare_and_fusion), kind=kLoop, calls=%fused_computation.9 | loop fusion | flops 12574720 | bytes 12649216 | tf_op jit(solution)/shard_map/reduce_sum | solution.py:98
  117.9 56.3 %all-gather.2.cloned.1.call-done = bf16[512,8192]{1,0:T(8,128)(2,1)} async-done(((bf16[16,8192]{1,0:T(8,128)(2,1)}), bf16[512,8192]{1,0:T(8,128)(2,1)}) %all-gather.2.cloned.1.call-update) | async-done | bytes 8388624 | tf_op jit(solution)/shard_map/all_gather | solution.py:47
  174.2 5.9 %fusion.50 = (bf16[512,4096]{1,0:T(8,128)(2,1)}, bf16[512,4096]{1,0:T(8,128)(2,1)}) fusion(bf16[512,8192]{1,0:T(8,128)(2,1)} %all-gather.2.cloned.1.call-done), kind=kLoop, calls=%fused_computation.84 | loop fusion | bytes 16777216 | tf_op jit(solution)/shard_map/split | solution.py:48
  180.2 6.5 %copy.109 = bf16[512,4096]{0,1:T(8,128)(2,1)} copy(bf16[512,4096]{1,0:T(8,128)(2,1)} %get-tuple-element.10) | data formatting | bytes 8388608 | tf_op jit(solution)/shard_map/split | solution.py:48
  186.7 6.4 %copy.105 = bf16[512,4096]{0,1:T(8,128)(2,1)} copy(bf16[512,4096]{1,0:T(8,128)(2,1)} %get-tuple-element.9) | data formatting | bytes 8388608 | tf_op jit(solution)/shard_map/split | solution.py:48
  193.1 11.5 %fusion.2 = (f32[2,32,128]{2,0,1:T(2,128)S(1)}, f32[32,512,2,128]{3,1,2,0:T(8,128)}) fusion(pred[2,128,512]{1,2,0:T(8,128)(4,1)S(1)} %broadcast_or_fusion, bf16[512,32,128,1]{0,2,3,1:T(8,128)(2,1)} %bitcast.99, bf16[2,128,32,128]{3,2,1,0:T(8,128)(2,1)S(1)} %bitcast.102), kind=kOutput, calls=%fused_computation.4 | convolution fusion | flops 1086316544 | bytes 23232512 | tf_op jit(solution)/shard_map/bqhd,jhd->bhqj/dot_general | solution.py:113
  204.6 8.4 %fusion = (f32[2,32,128]{2,0,1:T(2,128)S(1)}, bf16[2,32,128,512]{2,3,0,1:T(8,128)(2,1)S(1)}) fusion(f32[32,512,2,128]{3,1,2,0:T(8,128)} %get-tuple-element.22, f32[2,32,128]{2,0,1:T(2,128)S(1)} %copy.111, pred[2,128,512]{1,2,0:T(8,128)(4,1)S(1)} %broadcast_or_fusion), kind=kLoop, calls=%fused_computation.2 | loop fusion | flops 20963328 | bytes 25362432 | tf_op jit(solution)/shard_map/reduce_sum | solution.py:125
  213.0 6.8 %fusion.6 = f32[32,128,2,128]{1,3,0,2:T(8,128)} fusion(bf16[512,32,128,1]{0,2,1,3:T(8,128)(2,1)} %bitcast.98, bf16[2,32,128,512]{2,3,0,1:T(8,128)(2,1)S(1)} %get-tuple-element.8), kind=kOutput, calls=%fused_computation.11 | convolution fusion | flops 1073741824 | bytes 16777216 | tf_op jit(solution)/shard_map/bhqj,jhd->bhqd/dot_general | solution.py:126
  219.8 11.7 %fusion.30 = bf16[2,128,32,128]{3,1,2,0:T(8,128)(2,1)S(1)} fusion(f32[32,128,2,128]{1,3,0,2:T(8,128)} %fusion.6, bf16[1,128,32,128]{3,1,2,0:T(8,128)(2,1)S(1)} %copy-done.4, bf16[1,256,32,128]{3,1,2,0:T(8,128)(2,1)} %copy.101, bf16[1,128,32,128]{3,1,2,0:T(8,128)(2,1)} %copy.100, f32[2,32,384,128]{3,2,1,0:T(8,128)} %copy-done, ...), kind=kOutput, calls=%fused_computation.37 | convolution fusion | flops 847249408 | bytes 23167744 | tf_op jit(solution)/shard_map/bhqk,bkhd->bhqd/dot_general | solution.py:99
  231.5 1.4 copy.115
  232.8 2.3 copy.146
  (40 shorter events, 6.9 us)
Async XLA Ops:
  6.5 167.7 %all-gather.2.cloned.1.call-start = ((), (), s32[]{:S(2)}) async-start(), calls=%async_computation.1 | async-start | bytes 8650752 | tf_op jit(solution)/shard_map/all_gather | solution.py:47
  9.4 1.6 copy-start.1
  35.0 10.1 %copy-start.3 = (bf16[256,4096]{1,0:T(8,128)(2,1)S(1)}, bf16[256,4096]{1,0:T(8,128)(2,1)}, u32[]{:S(2)}) copy-start(bf16[256,4096]{1,0:T(8,128)(2,1)} %param.5) | copy-start | bytes 6291460
  36.6 50.7 %collective-permute-start.1 = (bf16[2,128,4096]{1,2,0:T(8,128)(2,1)}, bf16[2,128,4096]{1,2,0:T(8,128)(2,1)}, u32[]{:S(2)}, u32[]{:S(2)}) collective-permute-start(bf16[2,128,4096]{1,2,0:T(8,128)(2,1)} %pad_maximum_fusion.1), channel_id=1, source_target_pairs={{1,0},{2,1},{3,2},{4,3},{5,4},{6,5},{7,6},{8,7},{9,8},{10,9},{11,1... | collective-permute-start | bytes 6291464 | tf_op jit(solution)/shard_map/ppermute | solution.py:16
  43.0 51.3 %collective-permute-start = (bf16[2,128,4096]{1,2,0:T(8,128)(2,1)}, bf16[2,128,4096]{1,2,0:T(8,128)(2,1)}, u32[]{:S(2)}, u32[]{:S(2)}) collective-permute-start(bf16[2,128,4096]{1,2,0:T(8,128)(2,1)} %pad_maximum_fusion), channel_id=1, source_target_pairs={{0,1},{1,2},{2,3},{3,4},{4,5},{5,6},{6,7},{7,8},{8,9},{9,10},{10,1... | collective-permute-start | bytes 6291464 | tf_op jit(solution)/shard_map/ppermute | solution.py:16
  46.9 7.0 %copy-start.5 = (s32[2,32]{1,0:T(2,128)S(1)}, s32[2,32]{1,0:T(2,128)}, u32[]{:S(2)}) copy-start(s32[2,32]{1,0:T(2,128)} %param.9) | copy-start | bytes 772
  46.9 7.1 %copy-start.6 = (s32[2]{0:T(128)S(1)}, s32[2]{0:T(128)}, u32[]{:S(2)}) copy-start(s32[2]{0:T(128)} %param.8) | copy-start | bytes 28
  97.4 6.0 %copy-start.2 = (bf16[32,8,32,128]{3,2,1,0:T(8,128)(2,1)S(1)}, bf16[32,8,32,128]{3,2,1,0:T(8,128)(2,1)}, u32[]{:S(2)}) copy-start(bf16[32,8,32,128]{3,2,1,0:T(8,128)(2,1)} %copy.123) | copy-start | bytes 6291460
  109.6 4.6 %copy-start = (f32[2,32,384,128]{3,2,1,0:T(8,128)}, f32[2,32,384,128]{3,2,1,0:T(8,128)S(1)}, u32[]{:S(2)}) copy-start(f32[2,32,384,128]{3,2,1,0:T(8,128)S(1)} %get-tuple-element.20) | copy-start | bytes 37748740
  213.0 6.8 %copy-start.4 = (bf16[1,128,32,128]{3,1,2,0:T(8,128)(2,1)S(1)}, bf16[1,128,32,128]{3,1,2,0:T(8,128)(2,1)}, u32[]{:S(2)}) copy-start(bf16[1,128,32,128]{3,1,2,0:T(8,128)(2,1)} %copy.103) | copy-start | bytes 3145732
Sparse Core Ops, SparseCore 0:
  25.8 148.4 all-gather.1
where the time goes:
time: 243 us; the launch traced here: 242 us
  waiting for transfers between devices  93.3 us (38%)
  local copies, waits for them, and re-layouts  60.9 us (25%)
  matrix products  36 us (15%)
  other arithmetic  19.2 us (8%)
  between operations  13.6 us (6%)
  blocking collectives  11.9 us (5%)
  starting transfers between devices  7 us (3%)
    all_gather x1, waiting for transfers between devices, side_by_side(): result = lax.all_gather(both, axis, axis=dim, tiled=True)  56.3 us
    ppermute x2, waiting for transfers between devices, shifted(): return lax.ppermute(value, axis, pairs)  37 us
    split x3, local copies, waits for them, and re-layouts, side_by_side(): jnp.split(result, [sum(widths[:k]) for k in range(1, len(widths))], axis=...  18.9 us
    unnamed x20, local copies, waits for them, and re-layouts  18.7 us
    all_to_all x1, blocking collectives, copy_for_each(): return lax.all_to_all(copies, axis, split_axis=0, concat_axis=0, tiled=True)  11.9 us
    dot_general x1, matrix products, shards(): jnp.einsum('bhqk,bkhd->bhqd', weights.astype(jnp.bfloat16), window_values...  11.7 us
    dot_general x1, matrix products, shards(): jnp.einsum('bqhd,jhd->bhqj', query_blocks, piece_keys.reshape(length, HEA...  11.5 us
    reduce_sum x1, other arithmetic, shards(): totals_next = totals * factor + jnp.sum(part_weights, axis=-1)  8.4 us
  transfers between devices with their start and end apart: 3, of which 3 were waited for; matrix products, arithmetic and copies ran while one was open for 18% of the time, Pallas kernels for 0%

commit v1 on v0

v1 whole, which is shorter than its diff:
```python
import math

import jax
import jax.numpy as jnp
from jax import lax
from jax.experimental import pallas as pl
from jax.experimental.pallas import tpu as pltpu
from jax.sharding import PartitionSpec as P

HEADS = 32
HEAD_DIM = 128
BLOCK = 128
WIDTH = HEADS * HEAD_DIM
GROUPS = 32
SEQS = 8
ROWS = 2 * BLOCK
NBLK = 512
CHUNKS = 8
CHUNK_HEADS = HEADS // CHUNKS
CHUNK_WIDTH = WIDTH // CHUNKS
EARLY = 1
EXP_SCALE = math.log2(math.e) / math.sqrt(HEAD_DIM)
MESH = pl.DeviceIdType.MESH
NEG = float("-inf")


def kernel(
    gpos_ref, layout_ref, q_hbm, k_hbm, v_hbm, out_hbm,
    q_ref, k_ref, v_ref, lk_ref, lv_ref, rk_ref, rv_ref, first_ref, sk_ref, sv_ref, out_ref, bias_ref,
    load_sem, halo_send, halo_recv, first_send, first_recv, kz_send, kz_recv, vz_send, vz_recv,
    ky_send, ky_recv, vy_send, vy_recv, core_send, core_recv, out_sem,
):
    grp = lax.axis_index("grp")
    seq = lax.axis_index("seq")
    place = grp * SEQS + seq
    after = lax.rem(place + 1, GROUPS * SEQS)
    before = lax.rem(place + GROUPS * SEQS - 1, GROUPS * SEQS)
    z, y_hi, core = grp // 4, lax.rem(grp // 2, 2), lax.rem(grp, 2)
    y_lo, x = seq // 4, lax.rem(seq, 4)

    def group_at(dz, other_y=False, other_core=False):
        zz = lax.rem(z + dz + 8, 8)
        yy = 1 - y_hi if other_y else y_hi
        cc = 1 - core if other_core else core
        return (zz * 2 + yy) * 2 + cc

    right = (after // SEQS, lax.rem(after, SEQS))
    left = (before // SEQS, lax.rem(before, SEQS))
    x_peers = [(grp, y_lo * 4 + lax.rem(x + d, 4)) for d in (1, 3, 2)]
    y_peer = (grp, (1 - y_lo) * 4 + x)
    y_far = (group_at(0, other_y=True), (1 - y_lo) * 4 + x)
    z_up = (group_at(1), seq)
    z_down = (group_at(-1), seq)
    twin = (group_at(0, other_core=True), seq)

    barrier = pltpu.get_barrier_semaphore()
    partners = [left, right, *x_peers, y_peer, y_far, z_up, z_down, twin]
    for device in partners:
        pl.semaphore_signal(barrier, inc=1, device_id=device, device_id_type=MESH)

    loads = [
        pltpu.make_async_copy(src, dst, load_sem.at[n])
        for n, (src, dst) in enumerate(((k_hbm, k_ref), (v_hbm, v_ref), (q_hbm, q_ref)))
    ]
    for load in loads:
        load.start()
    pl.semaphore_wait(barrier, len(partners))

    def remote(src, dst, send, recv, device):
        return pltpu.make_async_remote_copy(
            src_ref=src, dst_ref=dst, send_sem=send, recv_sem=recv, device_id=device, device_id_type=MESH
        )

    last_rows, first_rows = pl.ds(BLOCK, BLOCK), pl.ds(0, BLOCK)

    def halo(c):
        lanes = pl.ds(pl.multiple_of(c * CHUNK_WIDTH, CHUNK_WIDTH), CHUNK_WIDTH)
        return [
            remote(k_hbm.at[last_rows, lanes], lk_ref.at[:, lanes], halo_send.at[0, c], halo_recv.at[0, c], right),
            remote(k_hbm.at[first_rows, lanes], rk_ref.at[:, lanes], halo_send.at[1, c], halo_recv.at[1, c], left),
            remote(v_hbm.at[last_rows, lanes], lv_ref.at[:, lanes], halo_send.at[2, c], halo_recv.at[2, c], right),
            remote(v_hbm.at[first_rows, lanes], rv_ref.at[:, lanes], halo_send.at[3, c], halo_recv.at[3, c], left),
        ]

    for c in range(EARLY):
        for copy in halo(c):
            copy.start()

    loads[0].wait()
    loads[1].wait()
    for h in range(HEADS):
        lanes = slice(h * HEAD_DIM, (h + 1) * HEAD_DIM)
        means = [
            jnp.sum(ref[b * BLOCK : (b + 1) * BLOCK, lanes].astype(jnp.float32), axis=0, keepdims=True)
            for ref in (k_ref, v_ref)
            for b in range(2)
        ]
        mean = jnp.concatenate(means, axis=0) * (1.0 / BLOCK)
        spread = jnp.mean(mean * mean, axis=-1, keepdims=True)
        first_ref[seq, :, lanes] = (mean / jnp.sqrt(spread + 1e-06)).astype(jnp.bfloat16)

    started = []

    def go(copy):
        copy.start()
        started.append(copy)
        return copy

    x_copies = [
        go(remote(first_ref.at[seq], first_ref.at[seq], first_send.at[n], first_recv.at[n], device))
        for n, device in enumerate(x_peers)
    ]
    for c in range(EARLY, CHUNKS):
        for copy in halo(c):
            copy.start()

    ids = lax.broadcasted_iota(jnp.int32, (1, NBLK), 1)
    rows = lax.broadcasted_iota(jnp.int32, (BLOCK, 1), 0)
    for b in range(2):
        listed = ids == layout_ref[b, 0]
        for n in range(1, layout_ref.shape[1]):
            listed = listed | (ids == layout_ref[b, n])
        bias = jnp.where(listed, 0.0, NEG)
        whole = jnp.where(rows == gpos_ref[b], 0.0, NEG)
        bias_ref[b * BLOCK : (b + 1) * BLOCK, :] = jnp.maximum(bias, whole)

    for copy in x_copies:
        copy.wait_recv()
    quad = pl.ds(y_lo * 4, 4)
    y_copy = go(remote(first_ref.at[quad], first_ref.at[quad], first_send.at[3], first_recv.at[3], y_peer))
    y_copy.wait_recv()

    def rows_of(group):
        return pl.ds(pl.multiple_of(group * 16, 16), 16)

    mine = rows_of(grp)
    for at, ref in ((0, sk_ref), (2, sv_ref)):
        pieces = [first_ref[d, at : at + 2, :].astype(jnp.float32) for d in range(SEQS)]
        ref[mine, :] = jnp.concatenate(pieces, axis=0).astype(jnp.bfloat16)

    def piece(ref, group, send, recv, device):
        return go(remote(ref.at[rows_of(group)], ref.at[rows_of(group)], send, recv, device))

    def arrived(ref, recv):
        pltpu.make_async_copy(ref.at[mine], ref.at[mine], recv).wait()

    cores = [0]

    def to_twin(ref, group, which):
        piece(ref, group, core_send.at[cores[0]], core_recv.at[which], twin)
        cores[0] += 1

    piece(sk_ref, grp, ky_send, ky_recv, y_far)
    piece(sv_ref, grp, vy_send.at[0], vy_recv.at[0], y_far)
    piece(sv_ref, grp, vz_send.at[0, 0], vz_recv.at[0, 0], z_up)
    piece(sv_ref, grp, vz_send.at[1, 0], vz_recv.at[1, 0], z_down)
    piece(sk_ref, grp, kz_send.at[0, 0], kz_recv.at[0, 0], z_up)
    piece(sk_ref, grp, kz_send.at[1, 0], kz_recv.at[1, 0], z_down)
    to_twin(sk_ref, grp, 0)
    to_twin(sv_ref, grp, 1)
    arrived(sk_ref, ky_recv)
    far = group_at(0, other_y=True)
    piece(sk_ref, far, kz_send.at[2, 0], kz_recv.at[2, 0], z_up)
    piece(sk_ref, far, kz_send.at[3, 0], kz_recv.at[3, 0], z_down)
    to_twin(sk_ref, far, 0)
    crossed = [(0, far)]
    for s in range(1, 5):
        for kind, (ref, send, recv, row, dz, steps) in enumerate((
            (sv_ref, vz_send, vz_recv, 0, -s, 4),
            (sv_ref, vz_send, vz_recv, 1, s, 3),
            (sk_ref, kz_send, kz_recv, 0, -s, 4),
            (sk_ref, kz_send, kz_recv, 1, s, 3),
            (sk_ref, kz_send, kz_recv, 2, -s, 3),
            (sk_ref, kz_send, kz_recv, 3, s, 4),
        )):
            if s > steps:
                continue
            group = group_at(dz, other_y=kind >= 4)
            arrived(ref, recv.at[row, s - 1])
            if s < steps:
                piece(ref, group, send.at[row, s], recv.at[row, s], z_up if row % 2 == 0 else z_down)
            if ref is sv_ref:
                n = 2 * s - 1 + row
                piece(ref, group, vy_send.at[n], vy_recv.at[n], y_far)
                crossed.append((n, group_at(dz, other_y=True)))
            to_twin(ref, group, 0 if ref is sk_ref else 1)
        while crossed and (crossed[0][0] < 2 * s - 1 or s == 4):
            n, group = crossed.pop(0)
            arrived(sv_ref, vy_recv.at[n])
            to_twin(sv_ref, group, 1)
    for which, ref in ((0, sk_ref), (1, sv_ref)):
        half = ref.at[pl.ds(0, NBLK // 2)]
        pltpu.make_async_copy(half, half, core_recv.at[which]).wait()

    loads[2].wait()
    bias_left = jnp.where(place == 0, NEG, 0.0)
    bias_right = jnp.where(place == GROUPS * SEQS - 1, NEG, 0.0)
    to_rows = (((1,), (1,)), ((), ()))
    to_cols = (((1,), (0,)), ((), ()))

    def dot(a, b, dims):
        return lax.dot_general(a, b, dims, preferred_element_type=jnp.float32)

    def chunk(c, carry):
        for copy in halo(c):
            copy.wait_recv()
        for n in range(CHUNK_HEADS):
            lanes = pl.ds(pl.multiple_of(c * CHUNK_WIDTH + n * HEAD_DIM, HEAD_DIM), HEAD_DIM)
            q = q_ref[:, lanes]
            s_near = dot(q, k_ref[:, lanes], to_rows)
            s_left = dot(q[:BLOCK], lk_ref[:, lanes], to_rows) + bias_left
            s_right = dot(q[BLOCK:], rk_ref[:, lanes], to_rows) + bias_right
            s_side = jnp.concatenate([s_left, s_right], axis=0)
            s_sum = dot(q, sk_ref[:, lanes], to_rows) + bias_ref[...]
            scores = jnp.concatenate([s_near, s_side, s_sum], axis=1)
            peak = jnp.max(scores, axis=1, keepdims=True)
            weights = jnp.exp2((scores - peak) * EXP_SCALE)
            total = jnp.sum(weights, axis=1, keepdims=True)
            rounded = weights.astype(jnp.bfloat16)
            acc = dot(rounded[:, :ROWS], v_ref[:, lanes], to_cols)
            side = rounded[:, ROWS : ROWS + BLOCK]
            acc += jnp.concatenate([
                dot(side[:BLOCK], lv_ref[:, lanes], to_cols),
                dot(side[BLOCK:], rv_ref[:, lanes], to_cols),
            ], axis=0)
            acc += dot(rounded[:, ROWS + BLOCK :], sv_ref[:, lanes], to_cols)
            out_ref[:, lanes] = (acc / total).astype(jnp.bfloat16)
        store(c).start()
        return carry

    def store(c):
        lanes = pl.ds(pl.multiple_of(c * CHUNK_WIDTH, CHUNK_WIDTH), CHUNK_WIDTH)
        return pltpu.make_async_copy(out_ref.at[:, lanes], out_hbm.at[:, lanes], out_sem.at[c])

    lax.fori_loop(0, CHUNKS, chunk, 0)
    for copy in started:
        copy.wait_send()
    for c in range(CHUNKS):
        for copy in halo(c):
            copy.wait_send()
        store(c).wait()


def shards(queries, keys, values, global_pos, layout):
    bf16 = jnp.bfloat16
    any_spec = pl.BlockSpec(memory_space=pl.ANY)
    smem_spec = pl.BlockSpec(memory_space=pltpu.SMEM)
    dma = pltpu.SemaphoreType.DMA
    return pl.pallas_call(
        kernel,
        out_shape=jax.ShapeDtypeStruct((ROWS, WIDTH), bf16),
        in_specs=[smem_spec, smem_spec, any_spec, any_spec, any_spec],
        out_specs=any_spec,
        scratch_shapes=[
            *[pltpu.VMEM((ROWS, WIDTH), bf16)] * 3,
            *[pltpu.VMEM((BLOCK, WIDTH), bf16)] * 4,
            pltpu.VMEM((SEQS, 4, WIDTH), bf16),
            *[pltpu.VMEM((NBLK, WIDTH), bf16)] * 2,
            pltpu.VMEM((ROWS, WIDTH), bf16),
            pltpu.VMEM((ROWS, NBLK), jnp.float32),
            dma((3,)), dma((4, CHUNKS)), dma((4, CHUNKS)), dma((4,)), dma((4,)),
            dma((4, 4)), dma((4, 4)), dma((2, 4)), dma((2, 4)),
            dma, dma, dma((8,)), dma((8,)), dma((32,)), dma((2,)), dma((CHUNKS,)),
        ],
        compiler_params=pltpu.CompilerParams(collective_id=0, has_side_effects=True),
    )(global_pos, layout, queries, keys, values)


def solution(mesh):
    rows = P(("grp", "seq"), None)
    in_specs = (rows, rows, rows, P(("grp", "seq")), rows)
    return jax.shard_map(shards, mesh=mesh, in_specs=in_specs, out_specs=rows, check_vma=False)
```

time: 243 us -> 122 us (0.50)
  Pallas kernels: 0 us -> 118 us
  waiting for transfers between devices: 93.3 us -> 0 us
  local copies, waits for them, and re-layouts: 60.9 us -> 3.13 us
  matrix products: 36 us -> 0 us
  other arithmetic: 19.2 us -> 0 us
  between operations: 13.6 us -> 0.01 us
  blocking collectives: 11.9 us -> 0 us
  starting transfers between devices: 7 us -> 0 us
    pallas_call x0 -> x1, Pallas kernels: none -> 118 us  [shards(): pl.pallas_call(kernel, out_shape=jax.ShapeDtypeStruct((ROWS, WIDTH), bf16...]
    all_gather x1 -> x0, waiting for transfers between devices: 56.3 us -> none  [side_by_side(): result = lax.all_gather(both, axis, axis=dim, tiled=True)]
    ppermute x2 -> x0, waiting for transfers between devices: 37 us -> none  [shifted(): return lax.ppermute(value, axis, pairs)]
    dot_general x4 -> x0, matrix products: 36 us -> none  [the longest x1 11.7 us: shards(): jnp.einsum('bhqk,bkhd->bhqd', weights.astype(jnp.bfloat16), window_values...]
    split x3 -> x0, local copies, waits for them, and re-layouts: 18.9 us -> none  [side_by_side(): jnp.split(result, [sum(widths[:k]) for k in range(1, len(widths))], axis=...]
    unnamed x20 -> x1, local copies, waits for them, and re-layouts: 18.7 us -> 3.13 us
    concatenate x6 -> x0, local copies, waits for them, and re-layouts: 14.3 us -> none  [the longest x3 7.86 us: shards(): wide_keys = jnp.concatenate([from_left[0], keys, from_right[0]], axis=0)]
    reduce_sum x6 -> x0, other arithmetic: 12.8 us -> none  [the longest x1 8.4 us: shards(): totals_next = totals * factor + jnp.sum(part_weights, axis=-1)]
  transfers between devices with their start and end apart: 3 -> 0, of which waited for: 3 -> 0; matrix products, arithmetic and copies ran while one was open for 18% -> 0% of each run, Pallas kernels for 0% -> 0%
where the time goes in v1:
time: 122 us
  Pallas kernels  118 us (97%)
  local copies, waits for them, and re-layouts  3.13 us (3%)
    pallas_call x1, Pallas kernels, shards(): pl.pallas_call(kernel, out_shape=jax.ShapeDtypeStruct((ROWS, WIDTH), bf16...  118 us
    unnamed x1, local copies, waits for them, and re-layouts  3.13 us

profile of v1, /device:TPU:1, one launch (start us, length us, event | category | flops | bytes accessed | tf_op | source)
XLA Modules:
  0.0 121.6 jit_solution(6880571887941799014)
XLA Ops:
  0.0 118.5 %shard_map.55 = bf16[256,4096]{1,0:T(8,128)(2,1)} custom-call(s32[2]{0:T(128)} %gpos_ref.1, s32[2,32]{1,0:T(2,128)} %layout_ref.1, bf16[256,4096]{1,0:T(8,128)(2,1)} %q_hbm.1, bf16[256,4096]{1,0:T(8,128)(2,1)} %k_hbm.1, bf16[256,4096]{1,0:T(8,128)(2,1)} %v_hbm.1), custom_call_target="tpu_custom_call" | custom-call | tf_op jit(solution)/shard_map/pallas_call | solution.py:249
  118.5 3.1 %copy.7 = bf16[256,4096]{1,0:T(8,128)(2,1)} copy(bf16[256,4096]{1,0:T(8,128)(2,1)} %shard_map.55) | data formatting | bytes 4194304
